TPU v7x, 128 devices: a whole 4x4x4 slice. The times are simulated.
128 devices in a mesh: ep: 8 (over x_lo, y), tp: 16 (over x_hi, z, core).
Axes of the slice: x: 4 (x_hi: 2, x_lo: 2; x = x_hi * 2 + x_lo), y: 4, z: 4, core: 2. Of those that a mesh axis runs over, the one named last changes fastest.
Arguments:
- tokens: bfloat16 [1024, 6144], P('ep'), may hold values from -6 to 6
- expert_ids: int32 [1024, 2], P('ep'), may hold values from 0 to 7, all different within a row; in each aligned block of 128 rows (0 to 127, 128 to 255, ...) at most 48 rows name the same one
- router: bfloat16 [6144, 8], replicated, may hold values from -0.078125 to 0.078125
- gate_weight: bfloat16 [8, 6144, 8192], P('ep', None, 'tp'), may hold values from -0.078125 to 0.078125
- up_weight: bfloat16 [8, 6144, 8192], P('ep', None, 'tp'), may hold values from -0.078125 to 0.078125
- down_weight: bfloat16 [8, 8192, 6144], P('ep', 'tp'), may hold values from -0.0625 to 0.0625
- keep_mask: int32 [1024, 6144], P('ep'), may hold values 0 or 1
Outputs:
- layer_out: bfloat16 [1024, 6144], P('ep')
Inputs may be any that keep to these rules, and one draw needn't show every extreme that they name: `expert_ids`: each row names two different experts. In the rows of one token block of 128 rows no expert is named more than 48 times, a bound that some block reaches.
All inputs are finite; a program needn't handle non-finite values. No bound on the sum of `keep_mask` on one device may be relied on, other than what follows from the above.
Results may differ from a plain program's by a relative error of at most 0.018.
Values may be sent and summed in bfloat16 or wider, within the bound.
A program may use at most 128 MiB of HBM per device.

v0:
```python
import jax
import jax.numpy as jnp
from jax import lax
from jax.sharding import PartitionSpec as P


def shards(tokens, expert_ids, router, gate_weight, up_weight, down_weight, keep_mask):
    experts = router.shape[1]
    tok_rows = tokens.shape[0]
    width_model = tokens.shape[1]
    capacity = 3 * tok_rows // experts
    groups = lax.axis_size("tp")
    share = capacity // groups
    logits = jnp.dot(tokens, router, preferred_element_type=jnp.float32)
    picked = jnp.take_along_axis(logits, expert_ids, axis=1)
    weight_first = jax.nn.sigmoid(picked[:, 0] - picked[:, 1])
    weight_second = jax.nn.sigmoid(picked[:, 1] - picked[:, 0])
    onehot = (expert_ids[:, :, None] == jnp.arange(experts, dtype=jnp.int32)[None, None, :]).astype(
        jnp.int32
    )
    onehot = onehot.reshape(tok_rows * 2, experts)
    ranks = jnp.cumsum(onehot, axis=0) - onehot
    slot = jnp.sum(ranks * onehot, axis=1).reshape(tok_rows, 2)
    place = slot * experts + expert_ids
    lines = jnp.arange(experts * capacity, dtype=jnp.int32)
    picker = ((place[None, :, 0] == lines[:, None]) | (place[None, :, 1] == lines[:, None])).astype(
        jnp.bfloat16
    )
    outgoing = jnp.dot(picker, tokens, preferred_element_type=jnp.float32).astype(jnp.bfloat16)
    outgoing = outgoing.reshape(capacity, experts, width_model)
    w_gate = gate_weight[0]
    w_up = up_weight[0]
    w_down = down_weight[0]
    arrived = lax.all_to_all(outgoing, "ep", split_axis=1, concat_axis=1, tiled=True)
    rows = arrived.reshape(capacity * experts, width_model)
    gate = jnp.dot(rows, w_gate, preferred_element_type=jnp.float32)
    up = jnp.dot(rows, w_up, preferred_element_type=jnp.float32)
    hidden = (jax.nn.silu(gate) * up).astype(jnp.bfloat16)
    summed = lax.psum_scatter(
        jnp.dot(hidden, w_down, preferred_element_type=jnp.float32).astype(jnp.bfloat16),
        "tp",
        scatter_dimension=0,
        tiled=True,
    )
    expert_out = summed.reshape(share, experts, width_model)
    back = lax.all_to_all(expert_out, "ep", split_axis=1, concat_axis=1, tiled=True)
    returned = lax.all_gather(back, "tp", axis=0, tiled=True)
    returned = returned.reshape(capacity * experts, width_model)
    first_rows = jnp.take(returned, place[:, 0], axis=0).astype(jnp.float32)
    second_rows = jnp.take(returned, place[:, 1], axis=0).astype(jnp.float32)
    combined = weight_first[:, None] * first_rows + weight_second[:, None] * second_rows
    return (combined * keep_mask.astype(jnp.float32) * 1.25).astype(jnp.bfloat16)


def solution(mesh):
    return jax.shard_map(
        shards,
        mesh=mesh,
        in_specs=(
            P("ep", None),
            P("ep", None),
            P(),
            P("ep", None, "tp"),
            P("ep", None, "tp"),
            P("ep", "tp", None),
            P("ep", None),
        ),
        out_specs=P("ep", None),
        check_vma=False,
    )
```

profile of v0, /device:TPU:1, one launch (start us, length us, event | category | flops | bytes accessed | tf_op | source)
XLA Modules:
  0.0 271.0 jit_solution(9002187958353605451)
XLA Ops:
  6.5 0.0 copy-start
  6.5 0.0 reduce-scatter.2.cloned.1.call-start
  6.5 0.9 copy.49
  7.4 0.1 eq.60
  7.6 0.1 eq.56
  7.7 0.6 reduce-window.6
  8.3 0.2 slice_reduce_fusion.2
  8.6 0.1 fusion.29
  8.7 0.1 mul.50
  8.8 0.2 slice_reduce_fusion.1
  9.0 0.0 copy-done
  9.0 0.0 slice-start
  9.1 1.4 fusion
  10.4 0.0 slice-start.1
  10.4 2.6 copy.52
  13.0 59.9 %all_to_all.10 = bf16[48,8,6144]{2,0,1:T(8,128)(2,1)S(1)} all-to-all(bf16[48,8,6144]{2,0,1:T(8,128)(2,1)S(1)} %copy.52), channel_id=1, replica_groups=mesh['ep'=8,'tp'=16] {'ep'}, dimensions={1} | all-to-all | bytes 9437184 | tf_op jit(solution)/shard_map/all_to_all | solution.py:34
  73.0 0.0 copy-start.1
  73.0 2.2 copy-done.1
  75.2 0.0 slice-done
  75.2 0.0 slice-done.1
  75.2 3.0 %fusion.4 = f32[384,512]{1,0:T(8,128)S(1)} fusion(bf16[1,6144,512]{2,1,0:T(8,128)(2,1)S(1)} %bitcast.53, bf16[48,8,6144]{2,0,1:T(8,128)(2,1)S(1)} %all_to_all.10), kind=kOutput, calls=%fused_computation.9 | convolution fusion | flops 2415919104 | bytes 11796480 | tf_op jit(solution)/shard_map/dot_general | solution.py:36
  78.1 13.6 %convolution_convert_fusion = bf16[384,6144]{1,0:T(8,128)(2,1)} fusion(bf16[1,512,6144]{2,1,0:T(8,128)(2,1)} %param.14, bf16[1,6144,512]{2,1,0:T(8,128)(2,1)} %param.13, bf16[48,8,6144]{2,0,1:T(8,128)(2,1)} %copy-done.1, f32[384,512]{1,0:T(8,128)S(1)} %fusion.4), kind=kOutput, calls=%fused_computation.3 | convolution fusion | flops 4835377152 | bytes 22806528 | tf_op jit(solution)/shard_map/dot_general | solution.py:40
  91.7 0.0 copy-start.3
  91.7 0.0 copy-start.2
  91.7 0.0 reduce-scatter.2.cloned.1.call-update
  91.8 0.0 all-gather.2.cloned.1.call-start
  91.8 83.2 %reduce-scatter.2.cloned.1.call-done = bf16[24,6144]{1,0:T(8,128)(2,1)} async-done(((bf16[384,6144]{1,0:T(8,128)(2,1)}), bf16[24,6144]{1,0:T(8,128)(2,1)}) %reduce-scatter.2.cloned.1.call-update) | async-done | bytes 294928 | tf_op jit(solution)/shard_map/reduce_scatter | solution.py:39
  175.1 1.2 copy.54
  176.3 10.6 %all_to_all.11 = bf16[3,8,6144]{2,0,1:T(4,128)(2,1)S(1)} all-to-all(bf16[3,8,6144]{2,0,1:T(4,128)(2,1)S(1)} %copy.54), channel_id=1, replica_groups=mesh['ep'=8,'tp'=16] {'ep'}, dimensions={1} | all-to-all | bytes 589824 | tf_op jit(solution)/shard_map/all_to_all | solution.py:46
  186.9 0.9 copy.55
  187.9 0.0 all-gather.2.cloned.1.call-update
  187.9 0.0 copy-done.3
  187.9 0.1 copy.47
  188.0 0.1 reshape.71
  188.2 0.0 copy-done.2
  188.2 0.5 fusion.32
  188.7 1.4 gather_fusion
  190.1 0.1 reshape.74
  190.2 0.1 copy.48
  190.4 55.8 %all-gather.2.cloned.1.call-done = bf16[48,8,6144]{2,1,0:T(8,128)(2,1)} async-done(((bf16[3,8,6144]{2,1,0:T(8,128)(2,1)}), bf16[48,8,6144]{2,1,0:T(8,128)(2,1)}) %all-gather.2.cloned.1.call-update) | async-done | bytes 4718608 | tf_op jit(solution)/shard_map/all_gather | solution.py:47
  246.1 5.9 %gather_fusion.1 = bf16[128,6144]{1,0:T(8,128)(2,1)S(1)} fusion(bf16[384,6144]{1,0:T(8,128)(2,1)} %bitcast.49, s32[1024]{0:T(1024)S(1)} %pad_clamp_fusion.1), kind=kCustom, calls=%fused_computation.clone | custom fusion | bytes 3146240 | tf_op jit(solution)/shard_map/jit(_take)/gather | solution.py:49
  252.1 7.1 %gather_fusion.2 = bf16[128,6144]{1,0:T(8,128)(2,1)} fusion(bf16[384,6144]{1,0:T(8,128)(2,1)} %bitcast.50, s32[1024]{0:T(1024)S(1)} %pad_clamp_fusion), kind=kCustom, calls=%fused_computation.1.clone | custom fusion | bytes 3146240 | tf_op jit(solution)/shard_map/jit(_take)/gather | solution.py:50
  259.2 5.0 %multiply_convert_fusion = bf16[128,6144]{1,0:T(8,128)(2,1)} fusion(s32[128,6144]{1,0:T(8,128)} %param.15, bf16[128,6144]{1,0:T(8,128)(2,1)} %gather_fusion.2, bf16[128,6144]{1,0:T(8,128)(2,1)S(1)} %gather_fusion.1, f32[128]{0:T(128)S(1)} %get-tuple-element.9, f32[128]{0:T(128)S(1)} %get-tuple-element.8, pred[128]{0:T(512)(128)(4,1)S(1)} %get-tuple-element.12, ...), kind=kLoop, calls=%fused_computation.15 | loop fusion | flops 8650752 | bytes 7865600 | tf_op jit(solution)/shard_map/convert_element_type | solution.py:52
  (13 shorter events, 0.1 us)
Async XLA Ops:
  6.5 2.5 copy-start
  6.5 168.5 %reduce-scatter.2.cloned.1.call-start = ((), (), s32[]{:S(2)}) async-start(), calls=%async_computation.3 | async-start | bytes 5013504 | tf_op jit(solution)/shard_map/reduce_scatter | solution.py:39
  9.0 66.1 %slice-start = ((s8[6291456]{0:T(1024)(128)(4,1)}), s8[4194304]{0:T(1024)(128)(4,1)S(1)}, s32[]{:S(2)}) async-start(s8[6291456]{0:T(1024)(128)(4,1)} %bitcast.52), calls=%async_computation.5 | async-start | bytes 8388608
  10.4 64.7 %slice-start.1 = ((s8[6291456]{0:T(1024)(128)(4,1)}), s8[2097152]{0:T(1024)(128)(4,1)S(1)}, s32[]{:S(2)}) async-start(s8[6291456]{0:T(1024)(128)(4,1)} %bitcast.52), calls=%async_computation.6 | async-start | bytes 4194304
  73.0 2.2 copy-start.1
  91.7 96.1 %copy-start.3 = (s32[128,2]{0,1:T(2,128)S(1)}, s32[128,2]{0,1:T(2,128)}, u32[]{:S(2)}) copy-start(s32[128,2]{0,1:T(2,128)} %param.10) | copy-start | bytes 3076
  91.7 96.4 %copy-start.2 = (bf16[6144,8]{0,1:T(8,128)(2,1)S(1)}, bf16[6144,8]{0,1:T(8,128)(2,1)}, u32[]{:S(2)}) copy-start(bf16[6144,8]{0,1:T(8,128)(2,1)} %param.11) | copy-start | bytes 294916
  91.8 154.4 %all-gather.2.cloned.1.call-start = ((), (), s32[]{:S(2)}) async-start(), calls=%async_computation.4 | async-start | bytes 5013504 | tf_op jit(solution)/shard_map/all_gather | solution.py:47
Sparse Core Ops, SparseCore 0:
  91.9 83.1 reduce-scatter.1
  188.0 58.0 all-gather.1
where the time goes:
time: 271 us
  waiting for transfers between devices  139 us (51%)
  blocking collectives  70.6 us (26%)
  local copies, waits for them, and re-layouts  23.5 us (9%)
  matrix products  18.4 us (7%)
  between operations  13.6 us (5%)
  other arithmetic  5.8 us (2%)
    reduce_scatter x1, waiting for transfers between devices, shards(): lax.psum_scatter(jnp.dot(hidden, w_down, preferred_element_type=jnp.float...  83.2 us
    all_to_all x1, blocking collectives, shards(): lax.all_to_all(outgoing, 'ep', split_axis=1, concat_axis=1, tiled=True)  59.9 us
    all_gather x1, waiting for transfers between devices, shards(): returned = lax.all_gather(back, 'tp', axis=0, tiled=True)  55.8 us
    dot_general x1, matrix products, shards(): jnp.dot(hidden, w_down, preferred_element_type=jnp.float32)  13.6 us
    all_to_all x1, blocking collectives, shards(): lax.all_to_all(expert_out, 'ep', split_axis=1, concat_axis=1, tiled=True)  10.6 us
    gather x1, local copies, waits for them, and re-layouts, shards(): second_rows = jnp.take(returned, place[:, 1], axis=0).astype(jnp.float32)  7.09 us
    gather x1, local copies, waits for them, and re-layouts, shards(): first_rows = jnp.take(returned, place[:, 0], axis=0).astype(jnp.float32)  5.94 us
  transfers between devices with their start and end apart: 2, of which 2 were waited for; matrix products, arithmetic and copies ran while one was open for 1% of the time, Pallas kernels for 0%

commit v1 on v0

v1 whole, which is shorter than its diff:
```python
import functools

import jax
import jax.numpy as jnp
from jax import lax
from jax.experimental import pallas as pl
from jax.experimental.pallas import tpu as pltpu
from jax.sharding import PartitionSpec as P

MESH = pl.DeviceIdType.MESH
BF16 = jnp.bfloat16
F32 = jnp.float32
N_EP, N_TP = 8, 16
N_Z = 4
GW = 512
HOPS = [(1, 2), (0, 2), (1, 1), (1, 3), (0, 1), (0, 3), (1, 0)]
Z_HOPS = [2, 1, 3]


def dot(a, b):
    return jnp.dot(a, b, preferred_element_type=F32)


def kernel(cap, ids_ref, tok_h, rt_h, wg_h, wu_h, wd_h, mk_h, out_ref,
           tok, rt, wg, wu, wd, mk, og, oq, xg, xq, gate, up, hid, sd, rd, tt, cb,
           lsem, g_s, g_r, q_s, q_r, z_s, z_r, dg_s, dg_r, dq_s, dq_r, rd_s, rd_r,
           m_s, m_r, a_s, a_r, da_s, da_r):
    ep = lax.axis_index("ep")
    tp = lax.axis_index("tp")
    xl, y = ep // 4, ep % 4
    xh, z, c = tp // 8, (tp // 2) % N_Z, tp % 2
    tok_rows, width = tok.shape
    qw = oq.shape[2]
    rows = N_EP * cap
    rw = width // 8
    hw = rw // 2

    def ep_at(a, b):
        return ((xl + a) % 2) * 4 + (y + b) % 4

    def tp_at(h, s, k):
        return ((xh + h) % 2) * 8 + ((z + s) % N_Z) * 2 + (c + k) % 2

    barrier = pltpu.get_barrier_semaphore()
    for a in range(2):
        for b in range(4):
            for h in range(2):
                for s in range(N_Z):
                    if a or b or h or s:
                        pl.semaphore_signal(barrier, inc=1, device_id=(ep_at(a, b), tp_at(h, s, 0)), device_id_type=MESH)
    pl.semaphore_signal(barrier, inc=1, device_id=(ep, tp_at(0, 0, 1)), device_id_type=MESH)

    piece = z * 2 + c
    out_col = pl.multiple_of(piece * rw + xh * hw, 128)
    loads = [
        pltpu.make_async_copy(tok_h, tok, lsem.at[0]),
        pltpu.make_async_copy(wg_h.at[0], wg, lsem.at[1]),
        pltpu.make_async_copy(wu_h.at[0], wu, lsem.at[2]),
        pltpu.make_async_copy(wd_h.at[0], wd, lsem.at[3]),
        pltpu.make_async_copy(rt_h, rt, lsem.at[4]),
        pltpu.make_async_copy(mk_h.at[:, pl.ds(out_col, hw)], mk, lsem.at[5]),
    ]
    for cp in loads:
        cp.start()

    ids = ids_ref[...]
    id0, id1 = ids[:, 0:1], ids[:, 1:2]
    lane = lax.broadcasted_iota(jnp.int32, (tok_rows, 128), 1)
    sub = lax.broadcasted_iota(jnp.int32, (tok_rows, 128), 0)
    oh0 = (lane == id0).astype(F32)
    oh1 = (lane == id1).astype(F32)
    rlane = lax.broadcasted_iota(jnp.int32, (tok_rows, tok_rows), 1)
    rsub = lax.broadcasted_iota(jnp.int32, (tok_rows, tok_rows), 0)
    before = (rlane < rsub).astype(BF16)
    count = dot(before, (oh0 + oh1).astype(BF16))
    place0 = id0.astype(F32) * cap + jnp.sum(count * oh0, axis=1, keepdims=True)
    place1 = id1.astype(F32) * cap + jnp.sum(count * oh1, axis=1, keepdims=True)
    eye = rlane == rsub
    row0 = jnp.sum(jnp.where(eye, place0, 0.0), axis=0, keepdims=True)
    row1 = jnp.sum(jnp.where(eye, place1, 0.0), axis=0, keepdims=True)
    line = lax.broadcasted_iota(jnp.int32, (rows, tok_rows), 0).astype(F32)
    picker = ((line == row0) | (line == row1)).astype(BF16)
    loads[0].wait()
    g_col = pl.multiple_of(piece * GW, 128)
    q_col = pl.multiple_of(8 * GW + c * qw, 128)
    og[...] = dot(picker, tok[:, pl.ds(g_col, GW)]).astype(BF16).reshape(N_EP, cap, GW)
    oq[...] = dot(picker, tok[:, pl.ds(q_col, qw)]).astype(BF16).reshape(N_EP, cap, qw)
    xg[piece, ep] = og[ep]
    xq[c, ep] = oq[ep]

    pl.semaphore_wait(barrier, 64)

    def remote(src, dst, ss, rs, e, t):
        return pltpu.make_async_remote_copy(src_ref=src, dst_ref=dst, send_sem=ss, recv_sem=rs, device_id=(e, t), device_id_type=MESH)

    def arrived(dst, rs):
        remote(dst, dst, rs, rs, ep, tp_at(0, 0, 1)).wait_recv()

    def sent(src, ss):
        remote(src, src, ss, ss, ep, tp_at(0, 0, 1)).wait_send()

    twin = tp_at(0, 0, 1)
    for a, b in HOPS:
        e = ep_at(a, b)
        remote(og.at[e], xg.at[piece, ep], g_s, g_r.at[ep], e, tp).start()
    for a, b in HOPS:
        e = ep_at(a, b)
        remote(oq.at[e], xq.at[c, ep], q_s, q_r.at[ep], e, tp).start()

    def spread(d):
        for s in Z_HOPS:
            remote(xg.at[piece, d], xg.at[piece, d], z_s, z_r.at[z, d], ep, tp_at(0, s, 0)).start()
        remote(xg.at[piece, d], xg.at[piece, d], dg_s, dg_r.at[z], ep, twin).start()

    spread(ep)
    remote(xq.at[c, ep], xq.at[c, ep], dq_s, dq_r, ep, twin).start()
    order = HOPS[::-1]
    sources = [ep] + [ep_at(-a, -b + 4) for a, b in order]
    for d in sources[1:]:
        arrived(xg.at[piece, d], g_r.at[d])
        spread(d)

    gate[...] = jnp.zeros_like(gate)
    up[...] = jnp.zeros_like(up)
    loads[1].wait()
    loads[2].wait()

    def consume(x, first, size):
        k = pl.ds(pl.multiple_of(first, 128), size)
        gate[...] += dot(x, wg[k, :])
        up[...] += dot(x, wu[k, :])

    def consume_g(p):
        consume(xg[p].reshape(rows, GW), p * GW, GW)

    consume_g(piece)
    other = z * 2 + (1 - c)
    arrived(xg.at[other], dg_r.at[z])
    consume_g(other)
    for s in Z_HOPS[::-1]:
        zz = (z + s) % N_Z
        for d in sources:
            arrived(xg.at[zz * 2 + c, d], z_r.at[zz, d])
            remote(xg.at[zz * 2 + c, d], xg.at[zz * 2 + c, d], dg_s, dg_r.at[zz], ep, twin).start()
    for d in sources[1:]:
        arrived(xq.at[c, d], q_r.at[d])
        remote(xq.at[c, d], xq.at[c, d], dq_s, dq_r, ep, twin).start()
    for s in Z_HOPS[::-1]:
        zz = (z + s) % N_Z
        consume_g(zz * 2 + c)
        arrived(xg.at[zz * 2 + 1 - c], dg_r.at[zz])
        consume_g(zz * 2 + 1 - c)
    consume(xq[c].reshape(rows, qw), 8 * GW + c * qw, qw)
    arrived(xq.at[1 - c], dq_r)
    consume(xq[1 - c].reshape(rows, qw), 8 * GW + (1 - c) * qw, qw)
    hid[...] = (jax.nn.silu(gate[...]) * up[...]).astype(BF16)
    loads[3].wait()

    z_order = Z_HOPS + [0]

    def down_twin(i):
        zz = (z + z_order[i]) % N_Z
        col = pl.multiple_of((zz * 2 + 1 - c) * rw, 128)
        sd[i] = dot(hid[...], wd[:, pl.ds(col, rw)]).astype(BF16)
        remote(sd.at[i], rd.at[i], rd_s, rd_r.at[i], ep, twin).start()

    def down_own(i):
        zz = (z + z_order[i]) % N_Z
        col = pl.multiple_of((zz * 2 + c) * rw, 128)
        arrived(rd.at[i], rd_r.at[i])
        total = dot(hid[...], wd[:, pl.ds(col, rw)]) + rd[i].astype(F32)
        tt[i] = total.astype(BF16).reshape(N_EP, cap, rw)
        for h in (1, 0):
            hcol = pl.multiple_of(((xh + h) % 2) * hw, 128)
            for a, b in HOPS + [(0, 0)]:
                e = ep_at(a, b)
                src = tt.at[i, e, :, pl.ds(hcol, hw)]
                here = (xh * N_Z + z) * N_EP + ep
                if h == 0 and a == 0 and b == 0 and z_order[i] == 0:
                    cb[here] = tt[i, e, :, pl.ds(hcol, hw)]
                else:
                    remote(src, cb.at[here], m_s, m_r, e, tp_at(h, z_order[i], 0)).start()

    down_twin(0)
    down_twin(1)
    down_own(0)
    down_twin(2)
    down_own(1)
    down_twin(3)
    down_own(2)
    down_own(3)

    loads[4].wait()
    loads[5].wait()
    logits = dot(tok[...], rt[...])
    elane = lax.broadcasted_iota(jnp.int32, logits.shape, 1)
    pick0 = jnp.sum(jnp.where(elane == id0, logits, 0.0), axis=1, keepdims=True)
    pick1 = jnp.sum(jnp.where(elane == id1, logits, 0.0), axis=1, keepdims=True)
    w0 = jax.nn.sigmoid(pick0 - pick1)
    w1 = jax.nn.sigmoid(pick1 - pick0)
    keep = mk[...].astype(F32) * 1.25
    cline = lax.broadcasted_iota(jnp.int32, (tok_rows, rows), 1).astype(F32)
    sel = jnp.concatenate([(cline == place0).astype(BF16), (cline == place1).astype(BF16)], axis=0)

    n_src = cb.shape[0]
    arrived(cb.at[pl.ds(0, n_src - 1)], m_r)
    total = cb[0:N_EP].astype(F32)
    for j in range(1, n_src // N_EP):
        total += cb[j * N_EP:(j + 1) * N_EP].astype(F32)
    both = dot(sel, total.astype(BF16).reshape(rows, hw))
    combined = w0 * both[:tok_rows] + w1 * both[tok_rows:]
    mine = pl.ds(out_col, hw)
    out_ref[:, mine] = (combined * keep).astype(BF16)

    for h in (1, 0):
        for s in Z_HOPS + [0]:
            if h or s:
                remote(out_ref.at[:, mine], out_ref.at[:, mine], a_s, a_r.at[xh * N_Z + z], ep, tp_at(h, s, 0)).start()
    remote(out_ref.at[:, mine], out_ref.at[:, mine], da_s, da_r, ep, twin).start()
    for h in (0, 1):
        for s in (0, 1, 3, 2):
            if h or s:
                hh, zz = (xh + h) % 2, (z + s) % N_Z
                theirs = pl.ds(pl.multiple_of((zz * 2 + c) * rw + hh * hw, 128), hw)
                arrived(out_ref.at[:, theirs], a_r.at[hh * N_Z + zz])
                remote(out_ref.at[:, theirs], out_ref.at[:, theirs], da_s, da_r, ep, twin).start()
    arrived(out_ref.at[:, pl.ds(0, 8 * hw)], da_r)

    sent(og.at[pl.ds(0, 7)], g_s)
    sent(oq.at[pl.ds(0, 7)], q_s)
    sent(xg.at[pl.ds(0, 3)], z_s)
    sent(xg.at[pl.ds(0, 4)], dg_s)
    sent(xq.at[0], dq_s)
    sent(sd, rd_s)
    sent(cb.at[pl.ds(0, n_src - 1)], m_s)
    sent(out_ref.at[:, pl.ds(0, 7 * hw)], a_s)
    sent(out_ref.at[:, pl.ds(0, 8 * hw)], da_s)


def shards(tokens, expert_ids, router, gate_weight, up_weight, down_weight, keep_mask):
    tok_rows, width = tokens.shape
    hidden = gate_weight.shape[2]
    cap = 3 * tok_rows // N_EP
    rows = N_EP * cap
    qw = (width - 8 * GW) // 2
    rw = width // 8
    hw = rw // 2
    any_spec = pl.BlockSpec(memory_space=pl.ANY)
    vmem_spec = pl.BlockSpec(memory_space=pltpu.VMEM)
    dma = pltpu.SemaphoreType.DMA
    return pl.pallas_call(
        functools.partial(kernel, cap),
        out_shape=jax.ShapeDtypeStruct((tok_rows, width), BF16),
        in_specs=[vmem_spec] + [any_spec] * 6,
        out_specs=vmem_spec,
        scratch_shapes=[
            pltpu.VMEM((tok_rows, width), BF16),
            pltpu.VMEM(router.shape, BF16),
            pltpu.VMEM((width, hidden), BF16),
            pltpu.VMEM((width, hidden), BF16),
            pltpu.VMEM((hidden, width), BF16),
            pltpu.VMEM((tok_rows, hw), jnp.int32),
            pltpu.VMEM((N_EP, cap, GW), BF16),
            pltpu.VMEM((N_EP, cap, qw), BF16),
            pltpu.VMEM((8, N_EP, cap, GW), BF16),
            pltpu.VMEM((2, N_EP, cap, qw), BF16),
            pltpu.VMEM((rows, hidden), F32),
            pltpu.VMEM((rows, hidden), F32),
            pltpu.VMEM((rows, hidden), BF16),
            pltpu.VMEM((N_Z, rows, rw), BF16),
            pltpu.VMEM((N_Z, rows, rw), BF16),
            pltpu.VMEM((N_Z, N_EP, cap, rw), BF16),
            pltpu.VMEM((8 * N_EP, cap, hw), BF16),
            dma((6,)),
            dma, dma((N_EP,)), dma, dma((N_EP,)),
            dma, dma((N_Z, N_EP)), dma, dma((N_Z,)), dma, dma,
            dma, dma((N_Z,)),
            dma, dma, dma, dma((8,)), dma, dma,
        ],
        compiler_params=pltpu.CompilerParams(
            collective_id=0, has_side_effects=True, vmem_limit_bytes=60 * 1024 * 1024
        ),
        name="expert_layer",
    )(expert_ids, tokens, router, gate_weight, up_weight, down_weight, keep_mask)


def solution(mesh):
    return jax.shard_map(
        shards,
        mesh=mesh,
        in_specs=(
            P("ep", None),
            P("ep", None),
            P(),
            P("ep", None, "tp"),
            P("ep", None, "tp"),
            P("ep", "tp", None),
            P("ep", None),
        ),
        out_specs=P("ep", None),
        check_vma=False,
    )
```

time: 271 us -> 100 us (0.37)
  waiting for transfers between devices: 139 us -> 0 us
  Pallas kernels: 0 us -> 93.6 us
  blocking collectives: 70.6 us -> 0 us
  matrix products: 18.4 us -> 0 us
  local copies, waits for them, and re-layouts: 23.5 us -> 6.33 us
  between operations: 13.6 us -> 0.01 us
  other arithmetic: 5.8 us -> 0 us
    pallas_call x0 -> x1, Pallas kernels: none -> 93.6 us  [shards(): pl.pallas_call(functools.partial(kernel, cap), out_shape=jax.ShapeDtypeSt...]
    reduce_scatter x1 -> x0, waiting for transfers between devices: 83.2 us -> none  [shards(): lax.psum_scatter(jnp.dot(hidden, w_down, preferred_element_type=jnp.float...]
    all_to_all x2 -> x0, blocking collectives: 70.6 us -> none  [the longest x1 59.9 us: shards(): lax.all_to_all(outgoing, 'ep', split_axis=1, concat_axis=1, tiled=True)]
    all_gather x1 -> x0, waiting for transfers between devices: 55.8 us -> none  [shards(): returned = lax.all_gather(back, 'tp', axis=0, tiled=True)]
    dot_general x4 -> x0, matrix products: 18.4 us -> none  [the longest x1 13.6 us: shards(): jnp.dot(hidden, w_down, preferred_element_type=jnp.float32)]
    gather x7 -> x0, local copies, waits for them, and re-layouts: 14.9 us -> none  [the longest x1 7.09 us: shards(): second_rows = jnp.take(returned, place[:, 1], axis=0).astype(jnp.float32)]
    convert_element_type x2 -> x0, other arithmetic: 5.01 us -> none  [the longest x1 5 us: shards(): (combined * keep_mask.astype(jnp.float32) * 1.25).astype(jnp.bfloat16)]
    reshape x2 -> x0, local copies, waits for them, and re-layouts: 3.8 us -> none  [the longest x1 2.59 us: shards(): outgoing = outgoing.reshape(capacity, experts, width_model)]
  transfers between devices with their start and end apart: 2 -> 0, of which waited for: 2 -> 0; matrix products, arithmetic and copies ran while one was open for 1% -> 0% of each run, Pallas kernels for 0% -> 0%
where the time goes in v1:
time: 100 us
  Pallas kernels  93.6 us (94%)
  local copies, waits for them, and re-layouts  6.33 us (6%)
    pallas_call x1, Pallas kernels, shards(): pl.pallas_call(functools.partial(kernel, cap), out_shape=jax.ShapeDtypeSt...  93.6 us
    unnamed x3, local copies, waits for them, and re-layouts  6.33 us

profile of v1, /device:TPU:1, one launch (start us, length us, event | category | flops | bytes accessed | tf_op | source)
XLA Modules:
  0.0 100.0 jit_solution(16492811514452375055)
XLA Ops:
  0.0 1.4 %copy.8.ids_ref = s32[128,2]{1,0:T(8,128)} copy(s32[128,2]{0,1:T(2,128)} %param.8) | data formatting | bytes 2048 | tf_op args[1]
  1.4 2.2 %copy.9.rt_h = bf16[6144,8]{1,0:T(8,128)(2,1)} copy(bf16[6144,8]{0,1:T(8,128)(2,1)} %param.9) | data formatting | bytes 196608 | tf_op args[2]
  3.6 93.6 %expert_layer.1 = bf16[128,6144]{1,0:T(8,128)(2,1)} custom-call(s32[128,2]{1,0:T(8,128)} %copy.8.ids_ref, bf16[128,6144]{1,0:T(8,128)(2,1)} %tok_h.1, bf16[6144,8]{1,0:T(8,128)(2,1)} %copy.9.rt_h, bf16[1,6144,512]{2,1,0:T(8,128)(2,1)} %wg_h.1, bf16[1,6144,512]{2,1,0:T(8,128)(2,1)} %wu_h.1, bf16[1,512,6144]{2,1,0:T(8,128)(2,1)} %wd_h.1, s32[128,6144]{1,0:T(8,128)} %mk_h.1), custom_call_target="tpu_custom_call" | custom-call | tf_op jit(solution)/shard_map/expert_layer/pallas_call | solution.py:251
  97.3 2.7 %copy.11 = bf16[128,6144]{1,0:T(8,128)(2,1)} copy(bf16[128,6144]{1,0:T(8,128)(2,1)} %expert_layer.1) | data formatting | bytes 3145728

commit v2 on v0

v2 whole, which is shorter than its diff:
```python
import functools

import jax
import jax.numpy as jnp
from jax import lax
from jax.experimental import pallas as pl
from jax.experimental.pallas import tpu as pltpu
from jax.sharding import PartitionSpec as P

MESH = pl.DeviceIdType.MESH
BF16 = jnp.bfloat16
F32 = jnp.float32
N_EP, N_TP = 8, 16
N_Z = 4
GW = 512
Z_HOPS = [2, 1, 3]
GROUPS = [[(0, 0), (1, 0), (0, 2), (1, 2)], [(0, 1), (0, 3), (1, 1), (1, 3)]]


def dot(a, b):
    return jnp.dot(a, b, preferred_element_type=F32)


def kernel(cap, ids_ref, tok_h, rt_h, wg_h, wu_h, wd_h, mk_h, out_ref,
           tok, rt, wg, wu, wd, mk, og, oq, xg, xq, gate, up, hid, sd, rd, tt, cb,
           lsem, g_s, g_r, q_s, q_r, z_s, z_r, dg_s, dg_r, dq_s, dq_r, rd_s, rd_r,
           m_s, m_r, a_s, a_r, da_s, da_r):
    ep = lax.axis_index("ep")
    tp = lax.axis_index("tp")
    xl, y = ep // 4, ep % 4
    xh, z, c = tp // 8, (tp // 2) % N_Z, tp % 2
    tok_rows, width = tok.shape
    qw = oq.shape[2]
    rows = N_EP * cap
    rw = width // 8
    hw = rw // 2

    def ep_at(a, b):
        return ((xl + a) % 2) * 4 + (y + b) % 4

    def tp_at(h, s, k):
        return ((xh + h) % 2) * 8 + ((z + s) % N_Z) * 2 + (c + k) % 2

    twin = tp_at(0, 0, 1)

    def remote(src, dst, ss, rs, e, t):
        return pltpu.make_async_remote_copy(src_ref=src, dst_ref=dst, send_sem=ss, recv_sem=rs, device_id=(e, t), device_id_type=MESH)

    def arrived(dst, rs):
        remote(dst, dst, rs, rs, ep, twin).wait_recv()

    def sent(src, ss):
        remote(src, src, ss, ss, ep, twin).wait_send()

    barrier = pltpu.get_barrier_semaphore()
    for a in range(2):
        for b in range(4):
            for h in range(2):
                for s in range(N_Z):
                    if a or b or h or s:
                        pl.semaphore_signal(barrier, inc=1, device_id=(ep_at(a, b), tp_at(h, s, 0)), device_id_type=MESH)
    pl.semaphore_signal(barrier, inc=1, device_id=(ep, twin), device_id_type=MESH)

    out_col = pl.multiple_of((z * 2 + c) * rw + xh * hw, 128)
    loads = [
        pltpu.make_async_copy(tok_h, tok, lsem.at[0]),
        pltpu.make_async_copy(wg_h.at[0], wg, lsem.at[1]),
        pltpu.make_async_copy(wu_h.at[0], wu, lsem.at[2]),
        pltpu.make_async_copy(wd_h.at[0], wd, lsem.at[3]),
        pltpu.make_async_copy(rt_h, rt, lsem.at[4]),
        pltpu.make_async_copy(mk_h.at[:, pl.ds(out_col, hw)], mk, lsem.at[5]),
    ]
    loads[0].start()

    with jax.named_scope("route"):
        ids = ids_ref[...].astype(F32)
        id0, id1 = ids[0:1, :], ids[1:2, :]
        esub = lax.broadcasted_iota(jnp.int32, (16, tok_rows), 0).astype(F32)
        oh0 = (esub == id0).astype(F32)
        oh1 = (esub == id1).astype(F32)
        rlane = lax.broadcasted_iota(jnp.int32, (tok_rows, tok_rows), 1)
        rsub = lax.broadcasted_iota(jnp.int32, (tok_rows, tok_rows), 0)
        before = (rsub < rlane).astype(BF16)
        count = dot((oh0 + oh1).astype(BF16), before)
        row0 = id0 * cap + jnp.sum(count * oh0, axis=0, keepdims=True)
        row1 = id1 * cap + jnp.sum(count * oh1, axis=0, keepdims=True)
        line = lax.broadcasted_iota(jnp.int32, (rows, tok_rows), 0).astype(F32)
        picker = ((line == row0) | (line == row1)).astype(BF16)
        loads[0].wait()
        for cp in loads[1:]:
            cp.start()
    with jax.named_scope("pick"):
        g_col = pl.multiple_of((z * 2 + c) * GW, 128)
        q_col = pl.multiple_of(8 * GW + c * qw, 128)
        og[...] = dot(picker, tok[:, pl.ds(g_col, GW)]).astype(BF16).reshape(N_EP, cap, GW)
        oq[...] = dot(picker, tok[:, pl.ds(q_col, qw)]).astype(BF16).reshape(N_EP, cap, qw)
        my_g = pl.ds(pl.multiple_of(c * GW, 128), GW)
        my_q = pl.ds(pl.multiple_of(c * qw, 128), qw)
        xg[z, ep, :, my_g] = og[ep]
        xq[ep, :, my_q] = oq[ep]
    with jax.named_scope("barrier"):
        pl.semaphore_wait(barrier, 64)

    for group in GROUPS:
        for a, b in group:
            if a or b:
                e = ep_at(a, b)
                remote(og.at[e], xg.at[z, ep, :, my_g], g_s, g_r.at[ep], e, tp).start()
        for a, b in group:
            if a or b:
                e = ep_at(a, b)
                remote(oq.at[e], xq.at[ep, :, my_q], q_s, q_r.at[ep], e, tp).start()

    def from_at(a, b):
        return ep_at(a, 4 - b)

    def spread(gi):
        for a, b in GROUPS[gi]:
            d = from_at(a, b)
            mine = xg.at[z, d, :, my_g]
            if a or b:
                arrived(mine, g_r.at[d])
            for s in Z_HOPS:
                remote(mine, mine, z_s, z_r.at[z, d], ep, tp_at(0, s, 0)).start()
            remote(mine, mine, dg_s, dg_r.at[gi, z], ep, twin).start()
            if not (a or b):
                remote(xq.at[d, :, my_q], xq.at[d, :, my_q], dq_s, dq_r.at[gi], ep, twin).start()

    def relay(gi):
        for a, b in GROUPS[gi]:
            d = from_at(a, b)
            for s in Z_HOPS[::-1]:
                zz = (z + s) % N_Z
                part = xg.at[zz, d, :, my_g]
                arrived(part, z_r.at[zz, d])
                remote(part, part, dg_s, dg_r.at[gi, zz], ep, twin).start()
        for a, b in GROUPS[gi]:
            d = from_at(a, b)
            if a or b:
                part = xq.at[d, :, my_q]
                arrived(part, q_r.at[d])
                remote(part, part, dq_s, dq_r.at[gi], ep, twin).start()

    def gather(ref, gi):
        return jnp.concatenate([ref[from_at(a, b)] for a, b in GROUPS[gi]], axis=0)

    def mlp(gi):
        n = len(GROUPS[gi])
        gate[...] = jnp.zeros_like(gate)
        up[...] = jnp.zeros_like(up)
        for s in [0] + Z_HOPS[::-1]:
            zz = (z + s) % N_Z
            arrived(xg.at[zz, pl.ds(0, n), :, my_g], dg_r.at[gi, zz])
            x = gather(xg.at[zz], gi)
            k = pl.ds(pl.multiple_of(zz * 2 * GW, 128), 2 * GW)
            gate[...] += dot(x, wg[k, :])
            up[...] += dot(x, wu[k, :])
        arrived(xq.at[pl.ds(0, n), :, my_q], dq_r.at[gi])
        x = gather(xq, gi)
        k = pl.ds(8 * GW, 2 * qw)
        total_gate = gate[...] + dot(x, wg[k, :])
        total_up = up[...] + dot(x, wu[k, :])
        hid[gi] = (jax.nn.silu(total_gate) * total_up).astype(BF16)

    z_order = Z_HOPS + [0]

    def down(gi):
        def down_twin(i):
            zz = (z + z_order[i]) % N_Z
            col = pl.multiple_of((zz * 2 + 1 - c) * rw, 128)
            sd[gi, i] = dot(hid[gi], wd[:, pl.ds(col, rw)]).astype(BF16)
            remote(sd.at[gi, i], rd.at[gi, i], rd_s, rd_r.at[gi, i], ep, twin).start()

        def down_own(i):
            zz = (z + z_order[i]) % N_Z
            col = pl.multiple_of((zz * 2 + c) * rw, 128)
            total = dot(hid[gi], wd[:, pl.ds(col, rw)])
            arrived(rd.at[gi, i], rd_r.at[gi, i])
            total = total + rd[gi, i].astype(F32)
            tt[gi, i] = total.astype(BF16).reshape(len(GROUPS[gi]), cap, rw)

        down_twin(0)
        down_twin(1)
        down_own(0)
        down_twin(2)
        down_own(1)
        down_twin(3)
        down_own(2)
        down_own(3)

    def scatter(gi):
        here = (xh * N_Z + z) * N_EP + ep
        n = len(GROUPS[gi])
        for t in range(4):
            for u in range(2):
                for v in range(4):
                    h = (v + u) % 2
                    i = (v + t) % 4
                    j = (v // 2 + t + u) % 2 * 2 + (v % 2) if n == 4 else 0
                    a, b = GROUPS[gi][j]
                    s = z_order[i]
                    d = from_at(a, b)
                    hcol = pl.multiple_of(((xh + h) % 2) * hw, 128)
                    if h or s or a or b:
                        remote(tt.at[gi, i, j, :, pl.ds(hcol, hw)], cb.at[here], m_s, m_r, d, tp_at(h, s, 0)).start()
                    else:
                        cb[here] = tt[gi, i, j, :, pl.ds(hcol, hw)]

    with jax.named_scope("spread0"):
        spread(0)
    with jax.named_scope("spread1"):
        spread(1)
    loads[1].wait()
    loads[2].wait()
    loads[3].wait()
    for gi in range(2):
        with jax.named_scope(f"relay{gi}"):
            relay(gi)
        with jax.named_scope(f"mlp{gi}"):
            mlp(gi)
        with jax.named_scope(f"down{gi}"):
            down(gi)
            scatter(gi)

    with jax.named_scope("gates"):
        loads[4].wait()
        loads[5].wait()
        logits = lax.dot_general(tok[...], rt[...], (((1,), (1,)), ((), ())), preferred_element_type=F32)
        eye = rlane == rsub

        def column(row):
            return jnp.sum(jnp.where(eye, row, 0.0), axis=1, keepdims=True)

        place0, place1 = column(row0), column(row1)
        elane = lax.broadcasted_iota(jnp.int32, logits.shape, 1).astype(F32)
        pick0 = jnp.sum(jnp.where(elane == column(id0), logits, 0.0), axis=1, keepdims=True)
        pick1 = jnp.sum(jnp.where(elane == column(id1), logits, 0.0), axis=1, keepdims=True)
        w0 = jax.nn.sigmoid(pick0 - pick1)
        w1 = jax.nn.sigmoid(pick1 - pick0)
        keep = mk[...].astype(F32) * 1.25
        cline = lax.broadcasted_iota(jnp.int32, (tok_rows, rows), 1).astype(F32)
        sel = jnp.concatenate([(cline == place0).astype(BF16), (cline == place1).astype(BF16)], axis=0)

    n_src = cb.shape[0]
    with jax.named_scope("m_wait"):
        arrived(cb.at[pl.ds(0, n_src - 1)], m_r)
    with jax.named_scope("combine"):
        total = cb[0:N_EP].astype(F32)
        for j in range(1, n_src // N_EP):
            total += cb[j * N_EP:(j + 1) * N_EP].astype(F32)
        both = dot(sel, total.astype(BF16).reshape(rows, hw))
        combined = w0 * both[:tok_rows] + w1 * both[tok_rows:]
        mine = pl.ds(out_col, hw)
        out_ref[:, mine] = (combined * keep).astype(BF16)

    with jax.named_scope("ag"):
        for h in (1, 0):
            for s in Z_HOPS + [0]:
                if h or s:
                    remote(out_ref.at[:, mine], out_ref.at[:, mine], a_s, a_r.at[xh * N_Z + z], ep, tp_at(h, s, 0)).start()
        remote(out_ref.at[:, mine], out_ref.at[:, mine], da_s, da_r, ep, twin).start()
        for h in (0, 1):
            for s in (0, 1, 3, 2):
                if h or s:
                    hh, zz = (xh + h) % 2, (z + s) % N_Z
                    theirs = pl.ds(pl.multiple_of((zz * 2 + c) * rw + hh * hw, 128), hw)
                    arrived(out_ref.at[:, theirs], a_r.at[hh * N_Z + zz])
                    remote(out_ref.at[:, theirs], out_ref.at[:, theirs], da_s, da_r, ep, twin).start()
        arrived(out_ref.at[:, pl.ds(0, 8 * hw)], da_r)

    sent(og.at[pl.ds(0, 7)], g_s)
    sent(oq.at[pl.ds(0, 7)], q_s)
    sent(xg.at[pl.ds(0, 3), :, :, my_g], z_s)
    sent(xg.at[:, :, :, my_g], dg_s)
    sent(oq, dq_s)
    sent(sd, rd_s)
    sent(cb.at[pl.ds(0, n_src - 1)], m_s)
    sent(out_ref.at[:, pl.ds(0, 7 * hw)], a_s)
    sent(out_ref.at[:, pl.ds(0, 8 * hw)], da_s)


def shards(tokens, expert_ids, router, gate_weight, up_weight, down_weight, keep_mask):
    tok_rows, width = tokens.shape
    hidden = gate_weight.shape[2]
    cap = 3 * tok_rows // N_EP
    rows = N_EP * cap
    qw = (width - 8 * GW) // 2
    rw = width // 8
    hw = rw // 2
    n_g = len(GROUPS)
    rows_g = rows // n_g
    any_spec = pl.BlockSpec(memory_space=pl.ANY)
    vmem_spec = pl.BlockSpec(memory_space=pltpu.VMEM)
    dma = pltpu.SemaphoreType.DMA
    return pl.pallas_call(
        functools.partial(kernel, cap),
        out_shape=jax.ShapeDtypeStruct((tok_rows, width), BF16),
        in_specs=[vmem_spec] + [any_spec] * 6,
        out_specs=vmem_spec,
        scratch_shapes=[
            pltpu.VMEM((tok_rows, width), BF16),
            pltpu.VMEM(router.shape[::-1], BF16),
            pltpu.VMEM((width, hidden), BF16),
            pltpu.VMEM((width, hidden), BF16),
            pltpu.VMEM((hidden, width), BF16),
            pltpu.VMEM((tok_rows, hw), jnp.int32),
            pltpu.VMEM((N_EP, cap, GW), BF16),
            pltpu.VMEM((N_EP, cap, qw), BF16),
            pltpu.VMEM((N_Z, N_EP, cap, 2 * GW), BF16),
            pltpu.VMEM((N_EP, cap, 2 * qw), BF16),
            pltpu.VMEM((rows_g, hidden), F32),
            pltpu.VMEM((rows_g, hidden), F32),
            pltpu.VMEM((n_g, rows_g, hidden), BF16),
            pltpu.VMEM((n_g, N_Z, rows_g, rw), BF16),
            pltpu.VMEM((n_g, N_Z, rows_g, rw), BF16),
            pltpu.VMEM((n_g, N_Z, N_EP // n_g, cap, rw), BF16),
            pltpu.VMEM((8 * N_EP, cap, hw), BF16),
            dma((6,)),
            dma, dma((N_EP,)), dma, dma((N_EP,)),
            dma, dma((N_Z, N_EP)), dma, dma((n_g, N_Z)), dma, dma((n_g,)),
            dma, dma((n_g, N_Z)),
            dma, dma, dma, dma((8,)), dma, dma,
        ],
        compiler_params=pltpu.CompilerParams(
            collective_id=0, has_side_effects=True, vmem_limit_bytes=52 * 1024 * 1024
        ),
        name="expert_layer",
    )(expert_ids.T, tokens, router.T, gate_weight, up_weight, down_weight, keep_mask)


def solution(mesh):
    return jax.shard_map(
        shards,
        mesh=mesh,
        in_specs=(
            P("ep", None),
            P("ep", None),
            P(),
            P("ep", None, "tp"),
            P("ep", None, "tp"),
            P("ep", "tp", None),
            P("ep", None),
        ),
        out_specs=P("ep", None),
        check_vma=False,
    )
```

time: 271 us -> 77.4 us (0.29)
  waiting for transfers between devices: 139 us -> 0 us
  Pallas kernels: 0 us -> 74.5 us
  blocking collectives: 70.6 us -> 0 us
  local copies, waits for them, and re-layouts: 23.5 us -> 2.72 us
  matrix products: 18.4 us -> 0 us
  between operations: 13.6 us -> 0.01 us
  other arithmetic: 5.8 us -> 0 us
    reduce_scatter x1 -> x0, waiting for transfers between devices: 83.2 us -> none  [shards(): lax.psum_scatter(jnp.dot(hidden, w_down, preferred_element_type=jnp.float...]
    pallas_call x0 -> x1, Pallas kernels: none -> 74.5 us  [shards(): pl.pallas_call(functools.partial(kernel, cap), out_shape=jax.ShapeDtypeSt...]
    all_to_all x2 -> x0, blocking collectives: 70.6 us -> none  [the longest x1 59.9 us: shards(): lax.all_to_all(outgoing, 'ep', split_axis=1, concat_axis=1, tiled=True)]
    all_gather x1 -> x0, waiting for transfers between devices: 55.8 us -> none  [shards(): returned = lax.all_gather(back, 'tp', axis=0, tiled=True)]
    dot_general x4 -> x0, matrix products: 18.4 us -> none  [the longest x1 13.6 us: shards(): jnp.dot(hidden, w_down, preferred_element_type=jnp.float32)]
    gather x7 -> x0, local copies, waits for them, and re-layouts: 14.9 us -> none  [the longest x1 7.09 us: shards(): second_rows = jnp.take(returned, place[:, 1], axis=0).astype(jnp.float32)]
    convert_element_type x2 -> x0, other arithmetic: 5.01 us -> none  [the longest x1 5 us: shards(): (combined * keep_mask.astype(jnp.float32) * 1.25).astype(jnp.bfloat16)]
    reshape x2 -> x0, local copies, waits for them, and re-layouts: 3.8 us -> none  [the longest x1 2.59 us: shards(): outgoing = outgoing.reshape(capacity, experts, width_model)]
  transfers between devices with their start and end apart: 2 -> 0, of which waited for: 2 -> 0; matrix products, arithmetic and copies ran while one was open for 1% -> 0% of each run, Pallas kernels for 0% -> 0%
where the time goes in v2:
time: 77.4 us; the launch traced here: 77.2 us
  Pallas kernels  74.5 us (96%)
  local copies, waits for them, and re-layouts  2.72 us (4%)
    pallas_call x1, Pallas kernels, shards(): pl.pallas_call(functools.partial(kernel, cap), out_shape=jax.ShapeDtypeSt...  74.5 us
    unnamed x5, local copies, waits for them, and re-layouts  2.72 us

profile of v2, /device:TPU:1, one launch (start us, length us, event | category | flops | bytes accessed | tf_op | source)
XLA Modules:
  0.0 77.2 jit_solution(15983736402934145860)
XLA Ops:
  0.0 0.0 copy-start
  0.0 0.9 %copy-done = bf16[6144,8]{0,1:T(8,128)(2,1)S(1)} copy-done((bf16[6144,8]{0,1:T(8,128)(2,1)S(1)}, bf16[6144,8]{0,1:T(8,128)(2,1)}, u32[]{:S(2)}) %copy-start) | copy-done | bytes 98328
  0.9 0.0 copy-start.1
  0.9 0.7 copy-done.1
  1.6 74.5 %expert_layer.1 = bf16[128,6144]{1,0:T(8,128)(2,1)S(1)} custom-call(s32[2,128]{1,0:T(2,128)S(1)} %bitcast.3, bf16[128,6144]{1,0:T(8,128)(2,1)} %tok_h.1, bf16[8,6144]{1,0:T(8,128)(2,1)S(1)} %bitcast.2, bf16[1,6144,512]{2,1,0:T(8,128)(2,1)} %wg_h.1, bf16[1,6144,512]{2,1,0:T(8,128)(2,1)} %wu_h.1, bf16[1,512,6144]{2,1,0:T(8,128)(2,1)} %wd_h.1, s32[128,6144]{1,0:T(8,128)} %mk_h.1), custom_call_target="tpu_custom_call" | custom-call | tf_op jit(solution)/shard_map/expert_layer/pallas_call | solution.py:295
  76.0 1.1 %copy.9 = bf16[128,6144]{1,0:T(8,128)(2,1)} copy(bf16[128,6144]{1,0:T(8,128)(2,1)S(1)} %expert_layer.1) | data formatting | bytes 3145728
Async XLA Ops:
  0.0 0.9 %copy-start = (bf16[6144,8]{0,1:T(8,128)(2,1)S(1)}, bf16[6144,8]{0,1:T(8,128)(2,1)}, u32[]{:S(2)}) copy-start(bf16[6144,8]{0,1:T(8,128)(2,1)} %param.9) | copy-start | bytes 294916
  0.9 0.7 copy-start.1

commit v3 on v2

v3 whole, which is shorter than its diff:
```python
import functools

import jax
import jax.numpy as jnp
from jax import lax
from jax.experimental import pallas as pl
from jax.experimental.pallas import tpu as pltpu
from jax.sharding import PartitionSpec as P

MESH = pl.DeviceIdType.MESH
BF16 = jnp.bfloat16
F32 = jnp.float32
N_EP, N_TP = 8, 16
N_Z = 4
GW = 512
Z_HOPS = [2, 1, 3]
NC = 512
GROUPS = [[(0, 0), (1, 0), (0, 2), (1, 2)], [(0, 1), (0, 3), (1, 1), (1, 3)]]
SENDS = ['g0', 'q0', 'g1', 'q1']
STEPS = [
    "s0", "gates0", "s1", "rz0", "rq0", "w0", "mlp0", "tw0", "ow0", "rz1", "rq1", "mlp1", "tw1", "ow1",
]


def dot(a, b):
    return jnp.dot(a, b, preferred_element_type=F32)


def kernel(cap, ids_h, tok_h, rt_h, wg_h, wu_h, wd_h, mk_h, out_ref,
           ids_ref, tok, rt, wgu, wd, mk, og, oq, xx, acc, hid, sd, rd, tt, cb, wt, sel,
           lsem, g_s, g_r, q_s, q_r, z_s, z_r, dg_s, dg_r, dq_s, dq_r, rd_s, rd_r,
           m_s, m_r, a_s, a_r, da_s, da_r):
    ep = lax.axis_index("ep")
    tp = lax.axis_index("tp")
    xl, y = ep // 4, ep % 4
    xh, z, c = tp // 8, (tp // 2) % N_Z, tp % 2
    tok_rows, width = tok.shape
    qw = oq.shape[2]
    rows = N_EP * cap
    rw = width // 8
    hw = rw // 2

    def ep_at(a, b):
        return ((xl + a) % 2) * 4 + (y + b) % 4

    def tp_at(h, s, k):
        return ((xh + h) % 2) * 8 + ((z + s) % N_Z) * 2 + (c + k) % 2

    def tp_z(zz):
        return xh * 8 + zz * 2 + c

    twin = tp_at(0, 0, 1)

    def remote(src, dst, ss, rs, e, t):
        return pltpu.make_async_remote_copy(src_ref=src, dst_ref=dst, send_sem=ss, recv_sem=rs, device_id=(e, t), device_id_type=MESH)

    def arrived(dst, rs):
        remote(dst, dst, rs, rs, ep, twin).wait_recv()

    def sent(src, ss):
        remote(src, src, ss, ss, ep, twin).wait_send()

    first_loads = [
        pltpu.make_async_copy(ids_h, ids_ref, lsem.at[6]),
        pltpu.make_async_copy(tok_h, tok, lsem.at[0]),
    ]
    for cp in first_loads:
        cp.start()

    barrier = pltpu.get_barrier_semaphore()
    for a in range(2):
        for b in range(4):
            for h in range(2):
                for s in range(N_Z):
                    if a or b or h or s:
                        pl.semaphore_signal(barrier, inc=1, device_id=(ep_at(a, b), tp_at(h, s, 0)), device_id_type=MESH)
    pl.semaphore_signal(barrier, inc=1, device_id=(ep, twin), device_id_type=MESH)

    out_col = pl.multiple_of((c * N_Z + z) * rw + xh * hw, 128)
    loads = [
        pltpu.make_async_copy(rt_h, rt, lsem.at[4]),
        pltpu.make_async_copy(mk_h.at[:, pl.ds(out_col, hw)], mk, lsem.at[5]),
        pltpu.make_async_copy(wg_h.at[0], wgu.at[0], lsem.at[1]),
        pltpu.make_async_copy(wu_h.at[0], wgu.at[1], lsem.at[2]),
        pltpu.make_async_copy(wd_h.at[0], wd, lsem.at[3]),
    ]
    with jax.named_scope("route"):
        first_loads[0].wait()
        ids = ids_ref[...].astype(F32)
        id0, id1 = ids[0:1, :], ids[1:2, :]
        esub = lax.broadcasted_iota(jnp.int32, (16, tok_rows), 0).astype(F32)
        oh0 = (esub == id0).astype(F32)
        oh1 = (esub == id1).astype(F32)
        rlane = lax.broadcasted_iota(jnp.int32, (tok_rows, tok_rows), 1)
        rsub = lax.broadcasted_iota(jnp.int32, (tok_rows, tok_rows), 0)
        before = (rsub < rlane).astype(BF16)
        count = dot((oh0 + oh1).astype(BF16), before)
        row0 = id0 * cap + jnp.sum(count * oh0, axis=0, keepdims=True)
        row1 = id1 * cap + jnp.sum(count * oh1, axis=0, keepdims=True)
        line = lax.broadcasted_iota(jnp.int32, (rows, tok_rows), 0).astype(F32)
        picker = ((line == row0) | (line == row1)).astype(BF16)
        first_loads[1].wait()
        for cp in loads:
            cp.start()
    with jax.named_scope("pick"):
        g_col = pl.multiple_of((z * 2 + c) * GW, 128)
        q_col = pl.multiple_of(8 * GW + c * qw, 128)
        og[...] = dot(picker, tok[:, pl.ds(g_col, GW)]).astype(BF16).reshape(N_EP, cap, GW)
        oq[...] = dot(picker, tok[:, pl.ds(q_col, qw)]).astype(BF16).reshape(N_EP, cap, qw)
        my_g = pl.ds(g_col, GW)
        my_q = pl.ds(q_col, qw)
        xx[ep, :, my_g] = og[ep]
        xx[ep, :, my_q] = oq[ep]
    with jax.named_scope("barrier"):
        pl.semaphore_wait(barrier, 64)

    def from_at(a, b):
        return ep_at(a, 4 - b)

    def spread_block(gi, d):
        mine = xx.at[d, :, my_g]
        for s in Z_HOPS:
            remote(mine, mine, z_s, z_r.at[z, d], ep, tp_at(0, s, 0)).start()
        remote(mine, mine, dg_s, dg_r.at[gi, z], ep, twin).start()

    def spread(gi):
        for a, b in GROUPS[gi]:
            if a or b:
                d = from_at(a, b)
                arrived(xx.at[d, :, my_g], g_r.at[d])
                spread_block(gi, d)

    spread_block(0, ep)
    for item in SENDS:
        for a, b in GROUPS[int(item[1])]:
            if a or b:
                e = ep_at(a, b)
                if item[0] == "g":
                    remote(og.at[e], xx.at[ep, :, my_g], g_s, g_r.at[ep], e, tp).start()
                else:
                    remote(oq.at[e], xx.at[ep, :, my_q], q_s, q_r.at[ep], e, tp).start()
    remote(xx.at[ep, :, my_q], xx.at[ep, :, my_q], dq_s, dq_r.at[0], ep, twin).start()

    def relay_z(gi):
        for a, b in GROUPS[gi]:
            d = from_at(a, b)
            for s in Z_HOPS[::-1]:
                zz = (z + s) % N_Z
                part = xx.at[d, :, pl.ds(pl.multiple_of((zz * 2 + c) * GW, 128), GW)]
                arrived(part, z_r.at[zz, d])
                remote(part, part, dg_s, dg_r.at[gi, zz], ep, twin).start()

    def relay_q(gi):
        for a, b in GROUPS[gi]:
            d = from_at(a, b)
            if a or b:
                part = xx.at[d, :, my_q]
                arrived(part, q_r.at[d])
                remote(part, part, dq_s, dq_r.at[gi], ep, twin).start()

    def mlp(gi):
        n = len(GROUPS[gi])
        for zz in range(N_Z):
            arrived(xx.at[pl.ds(0, n), :, my_g], dg_r.at[gi, zz])
        arrived(xx.at[pl.ds(0, n), :, my_q], dq_r.at[gi])
        blocks = [from_at(a, b) for a, b in GROUPS[gi]]

        def half(i, carry):
            x = jnp.concatenate([xx[d] for d in blocks], axis=0)
            acc[i, pl.ds(0, n * cap)] = dot(x, wgu[i])
            return carry

        lax.fori_loop(0, 2, half, 0)
        own_rows = pl.ds(0, n * cap)
        hid[gi, own_rows] = (jax.nn.silu(acc[0, own_rows]) * acc[1, own_rows]).astype(BF16)

    flip1, flip3 = z + 1 - 2 * (z % 2), 3 - z
    at, other = z % 2, 1 - z % 2

    def part_cols(f, q, hp):
        return pl.ds(pl.multiple_of((f * 2 + q) * rw + hp * hw, 128), hw)

    def cols(f, core, k):
        pair = (z // 2 + 1 + f) % 2
        return pl.ds(pl.multiple_of((core * 2 + pair) * 2 * rw + k * NC, 128), NC)

    def here(f, k):
        return pl.ds(pl.multiple_of(f * 2 * rw + k * NC, 128), NC)

    def down_twin(gi):
        own_rows = pl.ds(0, len(GROUPS[gi]) * cap)

        for f in range(2):
            def to_twin(k, carry):
                sd[gi, own_rows, here(f, k)] = dot(hid[gi, own_rows], wd[:, cols(f, 1 - c, k)]).astype(BF16)
                return carry

            lax.fori_loop(0, 2 * rw // NC, to_twin, 0)
            half = pl.ds(f * 2 * rw, 2 * rw)
            remote(sd.at[gi, own_rows, half], rd.at[gi, own_rows, half], rd_s, rd_r.at[gi, f], ep, twin).start()

    def down_own(gi):
        n = len(GROUPS[gi])
        own_rows = pl.ds(0, n * cap)
        slot = (xh * N_Z + z) * N_EP + ep
        for f in range(2):
            arrived(rd.at[gi, own_rows, pl.ds(f * 2 * rw, 2 * rw)], rd_r.at[gi, f])

            def own(k, carry):
                total = dot(hid[gi, own_rows], wd[:, cols(f, c, k)]) + rd[gi, own_rows, here(f, k)].astype(F32)
                tt[gi, pl.ds(0, n), :, here(f, k)] = total.astype(BF16).reshape(n, cap, NC)
                return carry

            lax.fori_loop(0, 2 * rw // NC, own, 0)
        for t in range(4):
            for j in range(n):
                for h in (1, 0):
                    r = (t + j + 2 * h) % 4
                    a, b = GROUPS[gi][j]
                    f, q, zz = [(0, at, (z + 2) % N_Z), (1, other, flip1), (0, other, flip3), (1, at, z)][r]
                    src = tt.at[gi, j, :, part_cols(f, q, (xh + h) % 2)]
                    if h or r < 3 or a or b:
                        to = ((xh + h) % 2) * 8 + zz * 2 + c
                        remote(src, cb.at[slot], m_s, m_r, from_at(a, b), to).start()
                    else:
                        cb[slot] = tt[gi, j, :, part_cols(f, q, xh)]

    def gates(_):
        loads[0].wait()
        loads[1].wait()
        logits = lax.dot_general(tok[...], rt[...], (((1,), (1,)), ((), ())), preferred_element_type=F32)
        eye = rlane == rsub

        def column(row):
            return jnp.sum(jnp.where(eye, row, 0.0), axis=1, keepdims=True)

        place0, place1 = column(row0), column(row1)
        elane = lax.broadcasted_iota(jnp.int32, logits.shape, 1).astype(F32)
        pick0 = jnp.sum(jnp.where(elane == column(id0), logits, 0.0), axis=1, keepdims=True)
        pick1 = jnp.sum(jnp.where(elane == column(id1), logits, 0.0), axis=1, keepdims=True)
        w0 = jax.nn.sigmoid(pick0 - pick1)
        w1 = jax.nn.sigmoid(pick1 - pick0)
        wt[0] = jnp.broadcast_to(w0, wt.shape[1:])
        wt[1] = jnp.broadcast_to(w1, wt.shape[1:])
        cline = lax.broadcasted_iota(jnp.int32, (tok_rows, rows), 1).astype(F32)
        sel[...] = jnp.concatenate([(cline == place0).astype(BF16), (cline == place1).astype(BF16)], axis=0)

    def weights(_):
        for cp in loads[2:]:
            cp.wait()

    work = {"gates": gates, "w": weights, "s": spread, "rz": relay_z, "rq": relay_q, "mlp": mlp, "tw": down_twin, "ow": down_own,}
    for step in STEPS:
        with jax.named_scope(step):
            work[step[:-1]](int(step[-1]))

    n_src = cb.shape[0]
    with jax.named_scope("m_wait"):
        arrived(cb.at[pl.ds(0, n_src - 1)], m_r)
    with jax.named_scope("combine"):
        total = cb[0:N_EP].astype(F32)
        for j in range(1, n_src // N_EP):
            total += cb[j * N_EP:(j + 1) * N_EP].astype(F32)
        both = dot(sel[...], total.astype(BF16).reshape(rows, hw))
        combined = wt[0, :, 0:1] * both[:tok_rows] + wt[1, :, 0:1] * both[tok_rows:]
        keep = mk[...].astype(F32) * 1.25
        mine = pl.ds(out_col, hw)
        out_ref[:, mine] = (combined * keep).astype(BF16)

    with jax.named_scope("ag"):
        def block(hh, zz):
            return out_ref.at[:, pl.ds(pl.multiple_of((c * N_Z + zz) * rw + hh * hw, 128), hw)]

        def share(hh, across):
            part = block(hh, z)
            if across:
                remote(part, part, a_s, a_r.at[hh * N_Z + z], ep, tp_at(1, 0, 0)).start()
            for s in Z_HOPS:
                remote(part, part, a_s, a_r.at[hh * N_Z + z], ep, tp_at(0, s, 0)).start()
            remote(part, part, da_s, da_r, ep, twin).start()

        def take(hh, zz):
            arrived(block(hh, zz), a_r.at[hh * N_Z + zz])

        share(xh, True)
        take(1 - xh, z)
        share(1 - xh, False)
        for hh in (xh, 1 - xh):
            for s in (1, 3, 2):
                zz = (z + s) % N_Z
                take(hh, zz)
                remote(block(hh, zz), block(hh, zz), da_s, da_r, ep, twin).start()
        arrived(out_ref.at[:, pl.ds(0, 8 * hw)], da_r)

    sent(og.at[pl.ds(0, 7)], g_s)
    sent(oq.at[pl.ds(0, 7)], q_s)
    sent(xx.at[:, :, pl.ds(0, 3 * GW)], z_s)
    sent(xx.at[:, :, pl.ds(0, 4 * GW)], dg_s)
    sent(oq, dq_s)
    for gi in range(len(GROUPS)):
        sent(sd.at[gi, pl.ds(0, len(GROUPS[gi]) * cap)], rd_s)
    sent(cb.at[pl.ds(0, n_src - 1)], m_s)
    sent(out_ref.at[:, pl.ds(0, 7 * hw)], a_s)
    sent(out_ref.at[:, pl.ds(0, 8 * hw)], da_s)


def shards(tokens, expert_ids, router, gate_weight, up_weight, down_weight, keep_mask):
    tok_rows, width = tokens.shape
    hidden = gate_weight.shape[2]
    cap = 3 * tok_rows // N_EP
    rows = N_EP * cap
    qw = (width - 8 * GW) // 2
    rw = width // 8
    hw = rw // 2
    n_g = len(GROUPS)
    n_max = max(len(group) for group in GROUPS)
    rows_g = n_max * cap
    hbm_spec = pl.BlockSpec(memory_space=pltpu.HBM)
    vmem_spec = pl.BlockSpec(memory_space=pltpu.VMEM)
    dma = pltpu.SemaphoreType.DMA
    return pl.pallas_call(
        functools.partial(kernel, cap),
        out_shape=jax.ShapeDtypeStruct((tok_rows, width), BF16),
        in_specs=[hbm_spec] * 7,
        out_specs=vmem_spec,
        scratch_shapes=[
            pltpu.VMEM((2, tok_rows), jnp.int32),
            pltpu.VMEM((tok_rows, width), BF16),
            pltpu.VMEM(router.shape[::-1], BF16),
            pltpu.VMEM((2, width, hidden), BF16),
            pltpu.VMEM((hidden, width), BF16),
            pltpu.VMEM((tok_rows, hw), jnp.int32),
            pltpu.VMEM((N_EP, cap, GW), BF16),
            pltpu.VMEM((N_EP, cap, qw), BF16),
            pltpu.VMEM((N_EP, cap, width), BF16),
            pltpu.VMEM((2, rows_g, hidden), F32),
            pltpu.VMEM((n_g, rows_g, hidden), BF16),
            pltpu.VMEM((n_g, rows_g, 4 * rw), BF16),
            pltpu.VMEM((n_g, rows_g, 4 * rw), BF16),
            pltpu.VMEM((n_g, n_max, cap, 4 * rw), BF16),
            pltpu.VMEM((8 * N_EP, cap, hw), BF16),
            pltpu.VMEM((2, tok_rows, 128), F32),
            pltpu.VMEM((2 * tok_rows, rows), BF16),
            dma((7,)),
            dma, dma((N_EP,)), dma, dma((N_EP,)),
            dma, dma((N_Z, N_EP)), dma, dma((n_g, N_Z)), dma, dma((n_g,)),
            dma, dma((n_g, 2)),
            dma, dma, dma, dma((8,)), dma, dma,
        ],
        compiler_params=pltpu.CompilerParams(
            collective_id=0, has_side_effects=True, vmem_limit_bytes=52 * 1024 * 1024
        ),
        name="expert_layer",
    )(expert_ids.T, tokens, router.T, gate_weight, up_weight, down_weight, keep_mask)


def solution(mesh):
    return jax.shard_map(
        shards,
        mesh=mesh,
        in_specs=(
            P("ep", None),
            P("ep", None),
            P(),
            P("ep", None, "tp"),
            P("ep", None, "tp"),
            P("ep", "tp", None),
            P("ep", None),
        ),
        out_specs=P("ep", None),
        check_vma=False,
    )
```

time: 77.4 us -> 76.3 us (0.986)
  Pallas kernels: 74.5 us -> 73.4 us
    pallas_call x1, Pallas kernels: 74.5 us -> 73.4 us  [shards(): pl.pallas_call(functools.partial(kernel, cap), out_shape=jax.ShapeDtypeSt...]
where the time goes in v3:
time: 76.3 us; the launch traced here: 76.1 us
  Pallas kernels  73.4 us (96%)
  local copies, waits for them, and re-layouts  2.72 us (4%)
    pallas_call x1, Pallas kernels, shards(): pl.pallas_call(functools.partial(kernel, cap), out_shape=jax.ShapeDtypeSt...  73.4 us
    unnamed x5, local copies, waits for them, and re-layouts  2.72 us

profile of v3, /device:TPU:1, one launch (start us, length us, event | category | flops | bytes accessed | tf_op | source)
XLA Modules:
  0.0 76.1 jit_solution(8608171883580564891)
XLA Ops:
  0.0 0.0 copy-start
  0.0 0.9 %copy-done = bf16[6144,8]{0,1:T(8,128)(2,1)S(1)} copy-done((bf16[6144,8]{0,1:T(8,128)(2,1)S(1)}, bf16[6144,8]{0,1:T(8,128)(2,1)}, u32[]{:S(2)}) %copy-start) | copy-done | bytes 98328
  0.9 0.0 copy-start.1
  0.9 0.7 copy-done.1
  1.6 73.4 %expert_layer.1 = bf16[128,6144]{1,0:T(8,128)(2,1)S(1)} custom-call(s32[2,128]{1,0:T(2,128)S(1)} %bitcast.3, bf16[128,6144]{1,0:T(8,128)(2,1)} %tok_h.1, bf16[8,6144]{1,0:T(8,128)(2,1)S(1)} %bitcast.2, bf16[1,6144,512]{2,1,0:T(8,128)(2,1)} %wg_h.1, bf16[1,6144,512]{2,1,0:T(8,128)(2,1)} %wu_h.1, bf16[1,512,6144]{2,1,0:T(8,128)(2,1)} %wd_h.1, s32[128,6144]{1,0:T(8,128)} %mk_h.1), custom_call_target="tpu_custom_call" | custom-call | tf_op jit(solution)/shard_map/expert_layer/pallas_call | solution.py:321
  75.0 1.1 %copy.9 = bf16[128,6144]{1,0:T(8,128)(2,1)} copy(bf16[128,6144]{1,0:T(8,128)(2,1)S(1)} %expert_layer.1) | data formatting | bytes 3145728
Async XLA Ops:
  0.0 0.9 %copy-start = (bf16[6144,8]{0,1:T(8,128)(2,1)S(1)}, bf16[6144,8]{0,1:T(8,128)(2,1)}, u32[]{:S(2)}) copy-start(bf16[6144,8]{0,1:T(8,128)(2,1)} %param.9) | copy-start | bytes 294916
  0.9 0.7 copy-start.1

commit v4 on v3

--- a/solution.py
+++ b/solution.py
@@ -16,7 +16,7 @@
 Z_HOPS = [2, 1, 3]
 NC = 512
 GROUPS = [[(0, 0), (1, 0), (0, 2), (1, 2)], [(0, 1), (0, 3), (1, 1), (1, 3)]]
-SENDS = ['g0', 'q0', 'g1', 'q1']
+SENDS = ['g0', 'g1', 'q0', 'q1']
 STEPS = [
     "s0", "gates0", "s1", "rz0", "rq0", "w0", "mlp0", "tw0", "ow0", "rz1", "rq1", "mlp1", "tw1", "ow1",
 ]

time: 76.3 us -> 75.4 us (0.988)
  Pallas kernels: 73.4 us -> 72.5 us
    pallas_call x1, Pallas kernels: 73.4 us -> 72.5 us  [shards(): pl.pallas_call(functools.partial(kernel, cap), out_shape=jax.ShapeDtypeSt...]
where the time goes in v4:
time: 75.4 us; the launch traced here: 75.2 us
  Pallas kernels  72.5 us (96%)
  local copies, waits for them, and re-layouts  2.72 us (4%)
    pallas_call x1, Pallas kernels, shards(): pl.pallas_call(functools.partial(kernel, cap), out_shape=jax.ShapeDtypeSt...  72.5 us
    unnamed x5, local copies, waits for them, and re-layouts  2.72 us

profile of v4, /device:TPU:1, one launch (start us, length us, event | category | flops | bytes accessed | tf_op | source)
XLA Modules:
  0.0 75.2 jit_solution(18008426526762875163)
XLA Ops:
  0.0 0.0 copy-start
  0.0 0.9 %copy-done = bf16[6144,8]{0,1:T(8,128)(2,1)S(1)} copy-done((bf16[6144,8]{0,1:T(8,128)(2,1)S(1)}, bf16[6144,8]{0,1:T(8,128)(2,1)}, u32[]{:S(2)}) %copy-start) | copy-done | bytes 98328
  0.9 0.0 copy-start.1
  0.9 0.7 copy-done.1
  1.6 72.5 %expert_layer.1 = bf16[128,6144]{1,0:T(8,128)(2,1)S(1)} custom-call(s32[2,128]{1,0:T(2,128)S(1)} %bitcast.3, bf16[128,6144]{1,0:T(8,128)(2,1)} %tok_h.1, bf16[8,6144]{1,0:T(8,128)(2,1)S(1)} %bitcast.2, bf16[1,6144,512]{2,1,0:T(8,128)(2,1)} %wg_h.1, bf16[1,6144,512]{2,1,0:T(8,128)(2,1)} %wu_h.1, bf16[1,512,6144]{2,1,0:T(8,128)(2,1)} %wd_h.1, s32[128,6144]{1,0:T(8,128)} %mk_h.1), custom_call_target="tpu_custom_call" | custom-call | tf_op jit(solution)/shard_map/expert_layer/pallas_call | solution.py:321
  74.1 1.1 %copy.9 = bf16[128,6144]{1,0:T(8,128)(2,1)} copy(bf16[128,6144]{1,0:T(8,128)(2,1)S(1)} %expert_layer.1) | data formatting | bytes 3145728
Async XLA Ops:
  0.0 0.9 %copy-start = (bf16[6144,8]{0,1:T(8,128)(2,1)S(1)}, bf16[6144,8]{0,1:T(8,128)(2,1)}, u32[]{:S(2)}) copy-start(bf16[6144,8]{0,1:T(8,128)(2,1)} %param.9) | copy-start | bytes 294916
  0.9 0.7 copy-start.1
